TPU v7x, 32 devices: a whole 2x2x4 slice. The times are simulated.
32 devices in a mesh: client: 32 (over z, y, x, core).
Axes of the slice: x: 2, y: 2, z: 4, core: 2. Of those that a mesh axis runs over, the one named last changes fastest.
Arguments:
- patches: bfloat16 [4096, 192], P('client'), may hold values from -6 to 6
- labels: int32 [256], replicated, may hold values from 0 to 9
- assign: int32 [32, 1], replicated, may hold values from 0 to 15; in each aligned block of 32 rows (0 to 31, 32 to 63, ...) at most 4 rows name the same one
- patch_embed: bfloat16 [192, 384], replicated, may hold values from -0.4375 to 0.4375
- positions: bfloat16 [16, 384], replicated, may hold values from -3 to 3
- client_in: bfloat16 [384, 3072], replicated, may hold values from -3 to 3
- client_down: bfloat16 [1536, 384], replicated, may hold values from -0.15625 to 0.15625
- server_in: bfloat16 [2, 6144, 3072], P(None, 'client'), may hold values from -3 to 3
- server_down: bfloat16 [2, 24576, 384], P(None, 'client'), may hold values from -0.15625 to 0.15625
- classifier: bfloat16 [16, 384, 10], replicated, may hold values from -15 to 15
Outputs:
- losses: float32 [32, 16], P('client')
- grad_patch_embed: float32 [192, 384], P(None, 'client')
- grad_positions: float32 [16, 384], P(None, 'client')
- grad_client_in: float32 [384, 3072], P(None, 'client')
- grad_client_down: float32 [1536, 384], P(None, 'client')
- grad_server_in: float32 [2, 6144, 3072], P(None, 'client')
- grad_server_down: float32 [2, 24576, 384], P(None, 'client')
- grad_classifier: float32 [6144, 10], P('client')
Inputs may be any that keep to these rules, and one draw needn't show every extreme that they name: `assign`: no server shard is named by more than 4 clients, a bound that some block reaches.
All inputs are finite; a program needn't handle non-finite values.
Results may differ from a plain program's by a relative error of at most 0.025.
Values may be sent and summed in bfloat16 or wider, within the bound.
No kernel may reach another device: no remote copies, remote signals or barrier semaphores. Data moves between devices by JAX's collectives and lax.ppermute only.
A program may use at most 128 MiB of HBM per device.

v0:
```python
import math

import jax
import jax.numpy as jnp
from jax import lax
from jax.sharding import PartitionSpec as P

D = 384
HEADS = 6
FF = 1536
TOK = 16
CLASSES = 10
IMG = 8
SHARDS = 16
SLOTS = 2
SERVER_LAYERS = 2


EPSILON = 1e-06


def partner_2(block, axis, apart):
    count = lax.axis_size(axis)
    route = []
    for low in range(count):
        high = low | 1 << apart
        if high != low and high < count:
            route += [(low, high), (high, low)]
    return lax.ppermute(block, axis, route)


def layer_norm(inputs):
    centre = inputs - jnp.mean(inputs, axis=-1, keepdims=True)
    spread = jnp.mean(centre * centre, axis=-1, keepdims=True)
    return centre * lax.rsqrt(spread + EPSILON)


def encoder_block(stream, weight_in, weight_down):
    images, tokens, model_width = stream.shape
    head_dim = model_width // HEADS
    normed = layer_norm(stream).astype(jnp.bfloat16).reshape(images * tokens, model_width)
    projected = jnp.dot(normed, weight_in[:, : 3 * model_width], preferred_element_type=jnp.float32)
    projected = projected.reshape(images, tokens, 3, HEADS, head_dim)
    queries = projected[:, :, 0]
    key_rows = projected[:, :, 1]
    values = projected[:, :, 2]
    scores = jnp.einsum(
        "bqhe,bkhe->bhqk", queries, key_rows, precision=lax.Precision.HIGHEST
    ) / math.sqrt(head_dim)
    weights_attn = jax.nn.softmax(scores, axis=-1)
    attended = jnp.einsum("bhqk,bkhe->bqhe", weights_attn, values, precision=lax.Precision.HIGHEST)
    attended = attended.reshape(images * tokens, model_width).astype(jnp.bfloat16)
    stream = stream + jnp.dot(
        attended,
        weight_in[:, 3 * model_width : 4 * model_width],
        preferred_element_type=jnp.float32,
    ).reshape(images, tokens, model_width)
    normed = layer_norm(stream).astype(jnp.bfloat16).reshape(images * tokens, model_width)
    hidden = jax.nn.gelu(
        jnp.dot(normed, weight_in[:, 4 * model_width :], preferred_element_type=jnp.float32)
    ).astype(jnp.bfloat16)
    return stream + jnp.dot(hidden, weight_down, preferred_element_type=jnp.float32).reshape(
        images, tokens, model_width
    )


def client_forward(patch_rows, patch_embed, positions, client_in, client_down):
    stream = jnp.dot(patch_rows, patch_embed, preferred_element_type=jnp.float32).reshape(
        -1, TOK, D
    )
    stream = stream + positions.astype(jnp.float32)
    stream = encoder_block(stream, client_in, client_down)
    return stream.reshape(-1, D).astype(jnp.bfloat16)


def server_loss(cut_rows, slot_hot, weights_in, weights_down, class_shard):
    stream = cut_rows.astype(jnp.float32).reshape(-1, TOK, D)
    for layer in range(len(weights_in)):
        stream = encoder_block(stream, weights_in[layer], weights_down[layer])
    pooled = layer_norm(jnp.mean(stream, axis=1)).astype(jnp.bfloat16)
    logits = jnp.dot(pooled, class_shard, preferred_element_type=jnp.float32)
    per_loss = (jax.nn.logsumexp(logits, axis=-1) - jnp.sum(slot_hot * logits, axis=-1)) * jnp.sum(
        slot_hot, axis=-1
    )
    return (jnp.sum(per_loss), per_loss)


def arrival_rank(routes):
    places = jnp.arange(routes.shape[0], dtype=jnp.int32)
    earlier = (routes[:, None] == routes[None, :]) & (places[:, None] < places[None, :])
    return jnp.sum(earlier.astype(jnp.int32), axis=0)


def select_matrix(routes, arrival, shard, capacity):
    slots_here = jnp.arange(capacity, dtype=jnp.int32)[:, None]
    return ((routes[None, :] == shard) & (arrival[None, :] == slots_here)).astype(jnp.bfloat16)


def slot_labels(labels, selector, rank_in_group, per_image, members):
    label_table = labels.reshape(members, IMG)
    label_part = lax.dynamic_slice_in_dim(label_table, rank_in_group * per_image, per_image, 1)
    onehot = (label_part[:, :, None] == jnp.arange(CLASSES, dtype=jnp.int32)[None, None, :]).astype(
        jnp.float32
    )
    onehot = onehot.reshape(members, per_image * CLASSES)
    chosen = jnp.dot(selector.astype(jnp.float32), onehot, precision=lax.Precision.HIGHEST)
    return chosen.reshape(-1, CLASSES)


def gather_group(flat_rows, group_bits, rank_in_group):
    stacked = flat_rows[None]
    for step_bit in range(group_bits):
        partner = partner_2(stacked, "client", step_bit)
        upper_half = rank_in_group >> step_bit & 1
        stacked = jnp.where(
            upper_half == 0,
            jnp.concatenate([stacked, partner], 0),
            jnp.concatenate([partner, stacked], 0),
        )
    return stacked


def reduce_group(blocks, group_bits, rank_in_group, order_bits):
    shaped = blocks.reshape((2,) * group_bits + (blocks.shape[1],))
    for step_bit in order_bits:
        axis_pos = group_bits - 1 - step_bit
        upper_half = rank_in_group >> step_bit & 1
        keeping = lax.dynamic_slice_in_dim(shaped, upper_half, 1, axis_pos)
        sending = lax.dynamic_slice_in_dim(shaped, 1 - upper_half, 1, axis_pos)
        shaped = keeping + partner_2(sending.astype(jnp.bfloat16), "client", step_bit).astype(
            sending.dtype
        )
    return shaped.reshape(-1)


def per_device(
    patches,
    labels,
    assign,
    patch_embed,
    positions,
    client_in,
    client_down,
    server_in,
    server_down,
    classifier,
):
    members = lax.axis_size("client")
    group_size = members // SHARDS
    group_bits = group_size.bit_length() - 1
    device_index = lax.axis_index("client")
    rank_in_group = device_index % group_size
    shard_here = device_index // group_size
    per_image = IMG // group_size
    piece_rows = IMG * TOK // group_size
    capacity = SLOTS * group_size
    width_all = 4 * D + FF
    rows_in = D // group_size
    rows_down = FF // group_size
    routes = assign[:, 0]
    places = jnp.arange(members, dtype=jnp.int32)
    own_shard = jnp.sum(jnp.where(places == device_index, routes, 0))

    def client_of(embed_weights, position_weights, in_weights, down_weights):
        return client_forward(patches, embed_weights, position_weights, in_weights, down_weights)

    cut_acts, client_back = jax.vjp(client_of, patch_embed, positions, client_in, client_down)
    pieces = cut_acts.reshape(group_size, piece_rows, D)
    tiled = jnp.broadcast_to(pieces[None], (SHARDS, group_size, piece_rows, D)).reshape(
        members, piece_rows, D
    )
    target = places // group_size == own_shard
    outgoing = jnp.where(target[:, None, None], tiled, jnp.zeros_like(tiled))
    arrived = lax.all_to_all(outgoing, "client", split_axis=0, concat_axis=0, tiled=True)
    arrival = arrival_rank(routes)
    selector = select_matrix(routes, arrival, shard_here, capacity)
    compact = jnp.dot(
        selector, arrived.reshape(members, piece_rows * D), preferred_element_type=jnp.float32
    )
    compact = compact.astype(jnp.bfloat16).reshape(capacity * piece_rows, D)
    slot_hot = slot_labels(labels, selector, rank_in_group, per_image, members)
    weights_in = []
    weights_down = []
    size_in = SERVER_LAYERS * rows_in * width_all
    flat_rows = jnp.concatenate([server_in.reshape(-1), server_down.reshape(-1)])
    stacked = gather_group(flat_rows, group_bits, rank_in_group)
    whole_in = stacked[:, :size_in].reshape(group_size, SERVER_LAYERS, rows_in, width_all)
    whole_in = whole_in.transpose(1, 0, 2, 3).reshape(SERVER_LAYERS, D, width_all)
    whole_down = stacked[:, size_in:].reshape(group_size, SERVER_LAYERS, rows_down, D)
    whole_down = whole_down.transpose(1, 0, 2, 3).reshape(SERVER_LAYERS, FF, D)
    for layer in range(SERVER_LAYERS):
        weights_in.append(whole_in[layer])
        weights_down.append(whole_down[layer])
    class_shard = lax.dynamic_index_in_dim(classifier, shard_here, 0, keepdims=False)

    def loss_of(cut_rows, list_in, list_down, class_weights):
        return server_loss(cut_rows, slot_hot, list_in, list_down, class_weights)

    total_loss, server_back, per_loss = jax.vjp(
        loss_of, compact, tuple(weights_in), tuple(weights_down), class_shard, has_aux=True
    )
    grad_cut, grad_in, grad_down, grad_class = server_back(jnp.ones((), jnp.float32))
    returning = jnp.dot(
        selector.T, grad_cut.reshape(capacity, piece_rows * D), preferred_element_type=jnp.float32
    )
    returning = returning.astype(jnp.bfloat16).reshape(members, piece_rows, D)
    returned = lax.all_to_all(returning, "client", split_axis=0, concat_axis=0, tiled=True)
    own_grads = lax.dynamic_slice_in_dim(returned, own_shard * group_size, group_size, 0)
    own_grads = own_grads.reshape(IMG * TOK, D)
    client_parts = client_back(own_grads)
    summed = lax.psum_scatter(
        tuple((part_grad.astype(jnp.float32) for part_grad in client_parts)),
        "client",
        scatter_dimension=1,
        tiled=True,
    )
    blocks_in = (
        jnp.stack(grad_in)
        .astype(jnp.float32)
        .reshape(SERVER_LAYERS, group_size, rows_in * width_all)
    )
    blocks_in = blocks_in.transpose(1, 0, 2).reshape(group_size, -1)
    blocks_down = (
        jnp.stack(grad_down).astype(jnp.float32).reshape(SERVER_LAYERS, group_size, rows_down * D)
    )
    blocks_down = blocks_down.transpose(1, 0, 2).reshape(group_size, -1)
    blocks_class = grad_class.astype(jnp.float32).reshape(group_size, rows_in * CLASSES)
    blocks = jnp.concatenate([blocks_in, blocks_down, blocks_class], 1)
    order_bits = list(range(group_bits - 1, -1, -1))
    own_sum = reduce_group(blocks, group_bits, rank_in_group, order_bits)
    size_in = SERVER_LAYERS * rows_in * width_all
    size_down = SERVER_LAYERS * rows_down * D
    grad_server_in = own_sum[:size_in].reshape(SERVER_LAYERS, rows_in, width_all)
    grad_server_down = own_sum[size_in : size_in + size_down].reshape(SERVER_LAYERS, rows_down, D)
    grad_classifier = own_sum[size_in + size_down :].reshape(rows_in, CLASSES)
    return (
        per_loss.reshape(1, -1),
        summed[0],
        summed[1],
        summed[2],
        summed[3],
        grad_server_in,
        grad_server_down,
        grad_classifier,
    )


def solution(mesh):
    in_specs = (
        P("client", None),
        P(),
        P(),
        P(),
        P(),
        P(),
        P(),
        P(None, "client", None),
        P(None, "client", None),
        P(),
    )
    out_specs = (
        P("client", None),
        P(None, "client"),
        P(None, "client"),
        P(None, "client"),
        P(None, "client"),
        P(None, "client", None),
        P(None, "client", None),
        P("client", None),
    )
    return jax.shard_map(
        per_device, mesh=mesh, in_specs=in_specs, out_specs=out_specs, check_vma=False
    )
```

profile of v0, /device:TPU:0, one launch (start us, length us, event | category | flops | bytes accessed | tf_op | source)
XLA Modules:
  0.0 716.9 jit_solution(912819160223898887)
XLA Ops:
  23.3 7.5 %all-to-all-start = ((bf16[32,64,384]{2,1,0:T(8,128)(2,1)}), bf16[32,64,384]{2,1,0:T(8,128)(2,1)S(1)}, u32[]{:S(2)}, u32[]{:S(2)}) async-start(bf16[32,64,384]{2,1,0:T(8,128)(2,1)} %bitcast_select_fusion), calls=%async_computation | async-start | bytes 3145728 | tf_op jit(solution)/shard_map/all_to_all | solution.py:174
  30.8 3.1 reshape.608
  36.2 10.4 %pad_maximum_fusion.1 = bf16[1769472]{0:T(1024)(128)(2,1)S(1)} fusion(bf16[589824]{0:T(1024)(128)(2,1)S(1)} %copy-done.16, bf16[1179648]{0:T(1024)(128)(2,1)S(1)} %bitcast.330), kind=kLoop, calls=%fused_computation.9 | loop fusion | flops 7077888 | bytes 7077888 | tf_op jit(solution)/shard_map/concatenate | solution.py:185
  46.6 41.6 %broadcast_in_dim.147 = bf16[1,1769472]{1,0:T(2,128)(2,1)} reshape(bf16[1769472]{0:T(1024)(128)(2,1)S(1)} %pad_maximum_fusion.1) | data formatting | bytes 7077888 | tf_op jit(solution)/shard_map/broadcast_in_dim | solution.py:111
  109.7 33.0 %broadcast_select_fusion = bf16[2,1769472]{1,0:T(2,128)(2,1)S(1)} fusion(pred[]{:T(512)S(6)} %eq.90, bf16[1,1769472]{1,0:T(2,128)(2,1)} %collective-permute-done, bf16[1,1769472]{1,0:T(2,128)(2,1)} %broadcast_in_dim.147), kind=kLoop, calls=%fused_computation.3 | loop fusion | flops 31850496 | bytes 14155777 | tf_op jit(solution)/shard_map/jit(_where)/select_n | solution.py:115
  142.8 3.3 slice.126
  146.1 3.4 slice.118
  170.8 3.2 multiply_convert_fusion.1
  211.2 2.8 reshape.618
  232.8 3.3 reshape.622
  250.1 4.9 stack.19
  271.0 4.8 stack.18
  277.9 5.8 all-to-all-start.1
  283.8 6.4 pad_maximum_fusion.2
  290.2 8.0 %pad_maximum_fusion = bf16[2,2,589824]{2,1,0:T(2,128)(2,1)} fusion(bf16[1,2,589824]{2,1,0:T(2,128)(2,1)S(1)} %copy-done.7, bf16[1,2,589824]{2,1,0:T(2,128)(2,1)S(1)} %copy-done.8), kind=kLoop, calls=%fused_computation.8 | loop fusion | flops 2359296 | bytes 9437184 | tf_op jit(solution)/shard_map/stack | solution.py:218
  298.2 56.1 %maximum_convert_fusion = f32[2,1771392]{1,0:T(2,128)S(1)} fusion(bf16[2,1920]{1,0:T(2,128)(2,1)S(1)} %copy-done.93, bf16[2,589824]{1,0:T(2,128)(2,1)} %bitcast.329, bf16[2,1179648]{1,0:T(2,128)(2,1)} %bitcast.326), kind=kLoop, calls=%fused_computation.4 | loop fusion | flops 21256704 | bytes 21256704 | tf_op jit(solution)/shard_map/concatenate | solution.py:228
  354.4 7.6 %dynamic-slice_convert_fusion = bf16[1,1771392]{1,0:T(2,128)(2,1)} fusion(f32[2,1771392]{1,0:T(2,128)S(1)} %maximum_convert_fusion, s32[]{:T(128)S(6)} %select_n.89), kind=kLoop, calls=%fused_computation.6 | loop fusion | bytes 7085572 | tf_op jit(solution)/shard_map/convert_element_type | solution.py:130
  367.1 82.9 %fusion = f32[1536,16]{0,1:T(8,128)S(1)} fusion(f32[1536,384]{0,1:T(8,128)} %fusion.2), kind=kCustom, calls=%all-reduce-scatter | all-reduce-scatter fusion | flops 786433 | bytes 2457600
  472.3 2.8 add_convert_fusion
  475.1 6.1 copy.141
  481.2 40.0 %all-reduce.19 = f32[16,384]{1,0:T(8,128)S(1)} all-reduce(bf16[16,384]{1,0:T(8,128)(2,1)S(1)} %get-tuple-element.42), channel_id=3, replica_groups=mesh['client'=32] {'client'}, use_global_device_ids=true, to_apply=%region_46.47.clone | all-reduce | flops 6144 | bytes 36864
  521.2 4.2 collective-permute-start.5
  526.7 3.4 collective-permute-start.3
  530.1 4.3 collective-permute-start.2
  535.1 3.8 concatenate.22
  539.5 55.7 %all-reduce.24.cloned.1.call-done = f32[192,384]{1,0:T(8,128)} async-done(((f32[192,384]{1,0:T(8,128)}), f32[192,384]{1,0:T(8,128)}) %all-reduce.24.cloned.1.call-update) | async-done | bytes 294928
  597.0 12.9 %convert_add_fusion = f32[1,1771392]{1,0:T(1,128)S(1)} fusion(bf16[1,1771392]{1,0:T(2,128)(2,1)} %collective-permute-done.1, f32[2,1771392]{1,0:T(2,128)} %copy-done.1, s32[]{:T(128)S(6)} %select_n.88), kind=kLoop, calls=%fused_computation.5 | loop fusion | flops 3542784 | bytes 17713924 | tf_op jit(solution)/shard_map/add | solution.py:130
  609.9 2.9 copy-done.2
  613.6 52.0 %slice_reduce_fusion = f32[1179648]{0:T(1024)} fusion(f32[1,1771392]{1,0:T(1,128)} %copy-done.2), kind=kLoop, calls=%fused_computation.7 | loop fusion | bytes 9437184 | tf_op jit(solution)/shard_map/slice | solution.py:233
  665.6 5.8 reshape.633
  671.4 25.4 %slice_reduce_fusion.1 = f32[589824]{0:T(1024)S(1)} fusion(f32[1,1771392]{1,0:T(1,128)} %copy-done.2), kind=kLoop, calls=%fused_computation.26 | loop fusion | bytes 4718592 | tf_op jit(solution)/shard_map/slice | solution.py:234
  698.5 11.2 %reduce-scatter.8.cloned.1.call-done = f32[96,384]{1,0:T(8,128)} async-done(((f32[3072,384]{1,0:T(8,128)}), f32[96,384]{1,0:T(8,128)}) %reduce-scatter.8.cloned.1.call-update) | async-done | bytes 147472
  (482 shorter events, 181.0 us)
Async XLA Ops:
  7.2 14.3 %copy-start = (bf16[1536,384]{1,0:T(8,128)(2,1)S(1)}, bf16[1536,384]{1,0:T(8,128)(2,1)}, u32[]{:S(2)}) copy-start(bf16[1536,384]{1,0:T(8,128)(2,1)} %param.16) | copy-start | bytes 3538948
  11.2 78.1 %copy-start.96 = (f32[128]{0:T(128)}, f32[128]{0:T(128)S(1)}, u32[]{:S(2)}) copy-start(f32[128]{0:T(128)S(1)} %broadcast_multiply_fusion.6) | copy-start | bytes 1540
  15.8 79.2 %copy-start.77 = (f32[8,6,16]{2,1,0:T(8,128)}, f32[8,6,16]{2,1,0:T(8,128)S(1)}, u32[]{:S(2)}) copy-start(f32[8,6,16]{2,1,0:T(8,128)S(1)} %fusion.73) | copy-start | bytes 9220
  23.3 72.4 %all-to-all-start = ((bf16[32,64,384]{2,1,0:T(8,128)(2,1)}), bf16[32,64,384]{2,1,0:T(8,128)(2,1)S(1)}, u32[]{:S(2)}, u32[]{:S(2)}) async-start(bf16[32,64,384]{2,1,0:T(8,128)(2,1)} %bitcast_select_fusion), calls=%async_computation | async-start | bytes 3145728 | tf_op jit(solution)/shard_map/all_to_all | solution.py:174
  46.6 44.4 %copy-start.109 = (s32[256]{0:T(256)S(1)}, s32[256]{0:T(256)}, u32[]{:S(2)}) copy-start(s32[256]{0:T(256)} %param.11) | copy-start | bytes 3076
  46.6 44.6 %copy-start.114 = (s32[32,1]{0,1:T(1,128)S(1)}, s32[32,1]{0,1:T(1,128)}, u32[]{:S(2)}) copy-start(s32[32,1]{0,1:T(1,128)} %param.12) | copy-start | bytes 388
  88.2 21.5 %collective-permute-start = (bf16[1,1769472]{1,0:T(2,128)(2,1)}, bf16[1,1769472]{1,0:T(2,128)(2,1)}, u32[]{:S(2)}, u32[]{:S(2)}) collective-permute-start(bf16[1,1769472]{1,0:T(2,128)(2,1)} %broadcast_in_dim.147), channel_id=1, source_target_pairs={{0,1},{1,0},{2,3},{3,2},{4,5},{5,4},{6,7},{7,6},{8,9},{9,8},{10,11... | collective-permute-start | bytes 10616840 | tf_op jit(solution)/shard_map/ppermute | solution.py:29
  186.1 12.0 %copy-start.64 = (f32[16,16]{1,0:T(8,128)}, f32[16,16]{1,0:T(8,128)S(1)}, u32[]{:S(2)}) copy-start(f32[16,16]{1,0:T(8,128)S(1)} %fusion.104) | copy-start | bytes 3076
  232.7 11.2 %copy-start.19 = (bf16[1536,384]{1,0:T(8,128)(2,1)S(1)}, bf16[1536,384]{1,0:T(8,128)(2,1)}, u32[]{:S(2)}) copy-start(bf16[1536,384]{1,0:T(8,128)(2,1)} %fusion.141) | copy-start | bytes 3538948
  255.0 8.8 %copy-start.76 = (f32[16,16]{1,0:T(8,128)S(1)}, f32[16,16]{1,0:T(8,128)}, u32[]{:S(2)}) copy-start(f32[16,16]{1,0:T(8,128)} %copy-done.75) | copy-start | bytes 3076
  258.3 10.0 %copy-start.22 = (bf16[384,1536]{1,0:T(8,128)(2,1)S(1)}, bf16[384,1536]{1,0:T(8,128)(2,1)}, u32[]{:S(2)}) copy-start(bf16[384,1536]{1,0:T(8,128)(2,1)} %fusion.144) | copy-start | bytes 3538948
  277.9 84.8 %all-to-all-start.1 = ((bf16[32,64,384]{2,1,0:T(8,128)(2,1)}), bf16[32,64,384]{2,1,0:T(8,128)(2,1)}, u32[]{:S(2)}, u32[]{:S(2)}) async-start(bf16[32,64,384]{2,1,0:T(8,128)(2,1)} %bitcast.137), calls=%async_computation.1 | async-start | bytes 3145728 | tf_op jit(solution)/shard_map/all_to_all | solution.py:207
  283.7 311.5 %all-reduce.24.cloned.1.call-start = ((), (), s32[]{:S(2)}) async-start(), calls=%async_computation.4 | async-start | bytes 589824
  290.2 8.0 %copy-start.93 = (bf16[2,1920]{1,0:T(2,128)(2,1)S(1)}, bf16[2,1920]{1,0:T(2,128)(2,1)}, u32[]{:S(2)}) copy-start(bf16[2,1920]{1,0:T(2,128)(2,1)} %reshape.632) | copy-start | bytes 23044
  354.3 7.9 %copy-start.99 = (f32[16]{0:T(128)S(1)}, f32[16]{0:T(128)}, u32[]{:S(2)}) copy-start(f32[16]{0:T(128)} %reduce_sum.472) | copy-start | bytes 196
  354.4 7.9 %copy-start.101 = (f32[16]{0:T(128)S(1)}, f32[16]{0:T(128)}, u32[]{:S(2)}) copy-start(f32[16]{0:T(128)} %copy-done.100) | copy-start | bytes 196
  354.4 9.3 %copy-start.33 = (f32[128,1536]{1,0:T(8,128)S(1)}, f32[128,1536]{1,0:T(8,128)}, u32[]{:S(2)}) copy-start(f32[128,1536]{1,0:T(8,128)} %copy-done.32) | copy-start | bytes 2359300
  362.0 234.9 %collective-permute-start.1 = (bf16[1,1771392]{1,0:T(2,128)(2,1)}, bf16[1,1771392]{1,0:T(2,128)(2,1)}, u32[]{:S(2)}, u32[]{:S(2)}) collective-permute-start(bf16[1,1771392]{1,0:T(2,128)(2,1)} %dynamic-slice_convert_fusion), channel_id=1, source_target_pairs={{0,1},{1,0},{2,3},{3,2},{4,5},{5,4},{6,7},{7,6},{8,9},{9,8},{10,11... | collective-permute-start | bytes 10628360 | tf_op jit(solution)/shard_map/ppermute | solution.py:29
  367.1 91.4 %copy-start.68 = (f32[8,16]{1,0:T(8,128)S(1)}, f32[8,16]{1,0:T(8,128)}, u32[]{:S(2)}) copy-start(f32[8,16]{1,0:T(8,128)} %copy-done.67) | copy-start | bytes 1540
  367.1 91.6 %copy-start.92 = (f32[8,16]{1,0:T(8,128)S(1)}, f32[8,16]{1,0:T(8,128)}, u32[]{:S(2)}) copy-start(f32[8,16]{1,0:T(8,128)} %copy-done.91) | copy-start | bytes 1540
  367.1 91.6 %copy-start.89 = (f32[8,16]{1,0:T(8,128)S(1)}, f32[8,16]{1,0:T(8,128)}, u32[]{:S(2)}) copy-start(f32[8,16]{1,0:T(8,128)} %copy-done.88) | copy-start | bytes 1540
  450.0 11.2 %copy-start.18 = (f32[8,16,3,6,64]{4,1,3,2,0:T(8,128)S(1)}, f32[8,16,3,6,64]{4,1,3,2,0:T(8,128)}, u32[]{:S(2)}) copy-start(f32[8,16,3,6,64]{4,1,3,2,0:T(8,128)} %copy-done.17) | copy-start | bytes 1769476
  450.0 11.2 %copy-start.30 = (f32[8,6,16,16]{2,3,1,0:T(8,128)S(1)}, f32[8,6,16,16]{2,3,1,0:T(8,128)}, u32[]{:S(2)}) copy-start(f32[8,6,16,16]{2,3,1,0:T(8,128)} %copy-done.29) | copy-start | bytes 147460
  450.7 74.7 %collective-permute-start.8 = (f32[1536,16]{0,1:T(8,128)S(1)}, f32[1536,16]{0,1:T(8,128)}, u32[]{:S(2)}, u32[]{:S(2)}) collective-permute-start(f32[1536,16]{0,1:T(8,128)S(1)} %fusion), channel_id=1, source_target_pairs={{0,7},{1,8},{2,9},{3,10},{4,11},{5,12},{6,13},{7,14},{8,15},{9,16}... | collective-permute-start | bytes 294920
  452.6 74.1 %collective-permute-start.7 = (f32[1536,16]{0,1:T(8,128)S(1)}, f32[1536,16]{0,1:T(8,128)}, u32[]{:S(2)}, u32[]{:S(2)}) collective-permute-start(f32[1536,16]{0,1:T(8,128)S(1)} %fusion), channel_id=1, source_target_pairs={{0,6},{1,7},{2,8},{3,9},{4,10},{5,11},{6,12},{7,13},{8,14},{9,15},... | collective-permute-start | bytes 294920
  454.5 75.6 %collective-permute-start.6 = (f32[1536,16]{0,1:T(8,128)S(1)}, f32[1536,16]{0,1:T(8,128)}, u32[]{:S(2)}, u32[]{:S(2)}) collective-permute-start(f32[1536,16]{0,1:T(8,128)S(1)} %fusion), channel_id=1, source_target_pairs={{0,5},{1,6},{2,7},{3,8},{4,9},{5,10},{6,11},{7,12},{8,13},{9,14},{... | collective-permute-start | bytes 294920
  469.7 240.0 %reduce-scatter.8.cloned.1.call-start = ((), (), s32[]{:S(2)}) async-start(), calls=%async_computation.3 | async-start | bytes 4866048
  469.8 51.4 %collective-permute-start.9 = (f32[1536,12]{0,1:T(8,128)S(1)}, f32[1536,12]{0,1:T(8,128)S(1)}, u32[]{:S(2)}, u32[]{:S(2)}) collective-permute-start(f32[1536,12]{0,1:T(8,128)S(1)} %copy-done.79), channel_id=1, source_target_pairs={{0,8},{1,9},{2,10},{3,11},{4,12},{5,13},{6,14},{7,15},{8,16},{9,17... | collective-permute-start | bytes 221192
  521.2 13.9 %collective-permute-start.5 = (f32[1536,16]{0,1:T(8,128)S(1)}, f32[1536,16]{0,1:T(8,128)S(1)}, u32[]{:S(2)}, u32[]{:S(2)}) collective-permute-start(f32[1536,16]{0,1:T(8,128)S(1)} %fusion), channel_id=1, source_target_pairs={{0,4},{1,5},{2,6},{3,7},{4,8},{5,9},{6,10},{7,11},{8,12},{9,13},{1... | collective-permute-start | bytes 294920
  525.4 9.7 %collective-permute-start.4 = (f32[1536,16]{0,1:T(8,128)S(1)}, f32[1536,16]{0,1:T(8,128)S(1)}, u32[]{:S(2)}, u32[]{:S(2)}) collective-permute-start(f32[1536,16]{0,1:T(8,128)S(1)} %fusion), channel_id=1, source_target_pairs={{0,3},{1,4},{2,5},{3,6},{4,7},{5,8},{6,9},{7,10},{8,11},{9,12},{10... | collective-permute-start | bytes 294920
  526.7 8.4 %collective-permute-start.3 = (f32[1536,16]{0,1:T(8,128)S(1)}, f32[1536,16]{0,1:T(8,128)S(1)}, u32[]{:S(2)}, u32[]{:S(2)}) collective-permute-start(f32[1536,16]{0,1:T(8,128)S(1)} %fusion), channel_id=1, source_target_pairs={{0,2},{1,3},{2,4},{3,5},{4,6},{5,7},{6,8},{7,9},{8,10},{9,11},{10,... | collective-permute-start | bytes 294920
  530.1 5.0 collective-permute-start.2
  (98 other events, 294.8 us)
Sparse Core Ops, SparseCore 0:
  469.8 125.3 all-reduce.23
  601.3 108.4 reduce-scatter.7
where the time goes:
time: 723 us; the launch traced here: 717 us
  local copies, waits for them, and re-layouts  242 us (33%)
  other arithmetic  157 us (22%)
  blocking collectives  123 us (17%)
  matrix products  75.8 us (10%)
  waiting for transfers between devices  67 us (9%)
  starting transfers between devices  34.4 us (5%)
  between operations  17.3 us (2%)
    unnamed x2, blocking collectives  123 us
    unnamed x12, waiting for transfers between devices  67 us
    concatenate x1, other arithmetic, per_device(): blocks = jnp.concatenate([blocks_in, blocks_down, blocks_class], 1)  56.1 us
    slice x1, local copies, waits for them, and re-layouts, per_device(): own_sum[:size_in].reshape(SERVER_LAYERS, rows_in, width_all)  52 us
    broadcast_in_dim x1, local copies, waits for them, and re-layouts, gather_group(): stacked = flat_rows[None]  41.6 us
    select_n x1, other arithmetic, gather_group(): jnp.where(upper_half == 0, jnp.concatenate([stacked, partner], 0), jnp.co...  33 us
    unnamed x249, local copies, waits for them, and re-layouts  32.7 us
    slice x1, local copies, waits for them, and re-layouts, per_device(): own_sum[size_in:size_in + size_down].reshape(SERVER_LAYERS, rows_down, D)  25.4 us
  transfers between devices with their start and end apart: 14, of which 2 were waited for; matrix products, arithmetic and copies ran while one was open for 52% of the time, Pallas kernels for 0%

commit v1 on v0

v1 whole, which is shorter than its diff:
```python
import math

import jax
import jax.numpy as jnp
from jax import lax
from jax.experimental import pallas as pl
from jax.experimental.pallas import tpu as pltpu
from jax.sharding import PartitionSpec as P

HEADS = 6
SHARDS = 16
SLOTS = 2
EPSILON = 1e-06
BF = jnp.bfloat16
F32 = jnp.float32
GELU_A = math.sqrt(2.0 / math.pi)
GELU_B = 0.044715
LANES = 128
ROWS16 = 16


def mm(a, b):
    return lax.dot_general(a, b, (((1,), (0,)), ((), ())), preferred_element_type=F32)


def mm_nt(a, b):
    return lax.dot_general(a, b, (((1,), (1,)), ((), ())), preferred_element_type=F32)


def mm_tn(a, b):
    return lax.dot_general(a, b, (((0,), (0,)), ((), ())), preferred_element_type=F32)


def norm_forward(x):
    centre = x - jnp.mean(x, axis=-1, keepdims=True)
    spread = jnp.mean(centre * centre, axis=-1, keepdims=True)
    scale = lax.rsqrt(spread + EPSILON)
    return centre * scale, scale


def norm_backward(grad, normed, scale):
    mean_grad = jnp.mean(grad, axis=-1, keepdims=True)
    mean_both = jnp.mean(grad * normed, axis=-1, keepdims=True)
    return scale * (grad - mean_grad - normed * mean_both)


def stage_orders(bits):
    even = list(range(1, bits))
    odd = [3, 1, 4, 2] if bits == 5 else even[len(even) // 2 :] + even[: len(even) // 2]
    return even, odd


def slot_of_chip(offset, core, bits):
    even, odd = stage_orders(bits)
    total = bits - 1

    def place(order):
        value = 0
        for step, bit in enumerate(order):
            value = value | (((offset >> (bit - 1)) & 1) << (total - 1 - step))
        return value

    return jnp.where(core == 0, place(even), place(odd))


def split_rows(x, mask):
    return jnp.concatenate([jnp.where(mask, x, 0.0), jnp.where(mask, 0.0, x)], axis=0)


def make_chain(cfg):
    d, ff, tok = cfg["d"], cfg["ff"], cfg["tok"]
    members, group, capacity, pr = cfg["members"], cfg["group"], cfg["capacity"], cfg["pr"]
    images, classes, patch = cfg["images"], cfg["classes"], cfg["patch"]
    layers, bits = cfg["layers"], cfg["bits"]
    rows = capacity * pr
    per_image = pr // tok
    rows_in, rows_down = d // group, ff // group
    cin, cin_pad = cfg["cin"], cfg["cin_pad"]
    chips = members // 2
    halves = rows // LANES
    pairs = d // LANES
    pieces = cfg["pieces"]
    dpc = d // members
    chunk = d
    packed = cfg["packed"]

    def kernel(*refs):
        (assign, labels, arrived, embed, positions, client_in, client_down), refs = refs[:7], refs[7:]
        piece_in, refs = refs[: len(pieces)], refs[len(pieces) :]
        piece_down, refs = refs[: len(pieces)], refs[len(pieces) :]
        classifier, refs = refs[0], refs[1:]
        (losses, dcls, keep_out, send_out), refs = refs[:4], refs[4:]
        saved_out, refs = refs[:8], refs[8:]
        (w_in, w_down, pat, slot, x_ref, y_ref, qkv_f, qkv_b, prob, gp, r1, r2), refs = (
            refs[:12],
            refs[12:],
        )
        saved_refs = refs[:8]
        (c_u, c_o, c_u2, c_h, c_dqkv, c_dy, c_dpre, c_dout, pcat, dob_pad, keep, send), refs = (
            refs[:12],
            refs[12:],
        )
        (sems,) = refs

        me = lax.axis_index("client")
        rank = me % group
        shard = me // group
        core = me % 2

        def weight_copies(layer):
            if layer == 0:
                return [
                    pltpu.make_async_copy(client_in, w_in.at[0], sems.at[0]),
                    pltpu.make_async_copy(client_down, w_down.at[0], sems.at[1]),
                ]
            out = []
            base = 2 + (layer - 1) * 2 * group
            for number, (src_in, src_down, first, count) in enumerate(
                zip(piece_in, piece_down, cfg["first"], pieces)
            ):
                for inner in range(count):
                    index = first + inner
                    owner = rank ^ index
                    at_in = pl.multiple_of(owner * rows_in, rows_in)
                    at_down = pl.multiple_of(owner * rows_down, rows_down)
                    out.append(
                        pltpu.make_async_copy(
                            src_in.at[inner, layer - 1],
                            w_in.at[layer, pl.ds(at_in, rows_in)],
                            sems.at[base + 2 * index],
                        )
                    )
                    out.append(
                        pltpu.make_async_copy(
                            src_down.at[inner, layer - 1],
                            w_down.at[layer, pl.ds(at_down, rows_down)],
                            sems.at[base + 2 * index + 1],
                        )
                    )
            return out

        first_other = 2 + (layers - 1) * 2 * group

        def saved_copies(layer):
            base = first_other + capacity + (layer - 1) * 8
            return [
                pltpu.make_async_copy(src.at[layer], dst.at[layer - 1], sems.at[base + i])
                for i, (src, dst) in enumerate(zip(saved_refs, saved_out))
            ]

        def grad_copies(number, first, count):
            base = first_other + capacity + (layers - 1) * 8 + 2 * number
            at = pl.ds(first, count)
            return [
                pltpu.make_async_copy(keep.at[:, at], keep_out.at[:, at], sems.at[base]),
                pltpu.make_async_copy(send.at[:, at], send_out.at[:, at], sems.at[base + 1]),
            ]

        for k in range(capacity):
            slot[k] = 0

        def scan(c, count):
            hit = (assign[c] == shard) & (count < capacity)

            @pl.when(hit)
            def _():
                slot[count] = c

            return count + hit.astype(jnp.int32)

        filled = lax.fori_loop(0, members, scan, jnp.int32(0))
        pat_copies = [
            pltpu.make_async_copy(arrived.at[slot[k]], pat.at[k], sems.at[first_other + k])
            for k in range(capacity)
        ]
        for copy in pat_copies:
            copy.start()
        for layer in range(layers):
            for copy in weight_copies(layer):
                copy.start()
        for copy in pat_copies:
            copy.wait()

        half_mask = lax.broadcasted_iota(jnp.int32, (LANES, LANES), 1) < LANES // 2
        width_slot = LANES // group
        lane = lax.broadcasted_iota(jnp.int32, (packed, LANES), 1)
        for v in range(halves):
            blocks = [pat[v * group + t].astype(F32) for t in range(group)]
            for part in range(group):
                value = blocks[0]
                for t in range(group):
                    moved = pltpu.roll(blocks[t], (width_slot * (t - part)) % LANES, 1)
                    value = jnp.where(lane // width_slot == t, moved, value)
                pcat[part * packed : (part + 1) * packed, v * LANES : (v + 1) * LANES] = value.astype(BF)
        token = lax.broadcasted_iota(jnp.int32, (tok, rows), 1) % tok
        pcat[patch:] = (token == lax.broadcasted_iota(jnp.int32, (tok, rows), 0)).astype(F32).astype(BF)
        x_ref[...] = mm_tn(pcat[...], jnp.concatenate([embed[...], positions[...]], axis=0))

        row_slot = lax.broadcasted_iota(jnp.int32, (rows, 1), 0) // pr
        col_block = lax.broadcasted_iota(jnp.int32, (2 * LANES, LANES), 1) // tok
        row_block = (lax.broadcasted_iota(jnp.int32, (2 * LANES, LANES), 0) % LANES) // tok
        block_mask = col_block == row_block

        def forward(layer, carry):
            for which in range(layers):

                @pl.when(layer == which)
                def _(which=which):
                    for copy in weight_copies(which):
                        copy.wait()

            x = x_ref[...]
            normed, scale = norm_forward(x)
            u = normed.astype(BF)
            c_u[layer] = u
            r1[layer] = scale
            for part in range(3):
                value = mm(u, w_in[layer, :, part * d : (part + 1) * d])
                qkv_f[:, part * d : (part + 1) * d] = value
                qkv_b[layer, :, part * d : (part + 1) * d] = value.astype(BF)
            head_dim = d // HEADS
            for g in range(halves):
                rs = slice(g * LANES, (g + 1) * LANES)
                for p in range(pairs):
                    q = qkv_f[rs, p * LANES : (p + 1) * LANES] * (1.0 / math.sqrt(head_dim))
                    k = qkv_f[rs, d + p * LANES : d + (p + 1) * LANES]
                    v = qkv_b[layer, rs, 2 * d + p * LANES : 2 * d + (p + 1) * LANES].astype(F32)
                    q2 = split_rows(q, half_mask)
                    q_hi = q2.astype(BF)
                    q_lo = (q2 - q_hi.astype(F32)).astype(BF)
                    k_hi = k.astype(BF)
                    k_lo = (k - k_hi.astype(F32)).astype(BF)
                    scores = mm_nt(
                        jnp.concatenate([q_hi, q_lo], 1), jnp.concatenate([k_hi, k_hi], 1)
                    ) + mm_nt(q_hi, k_lo)
                    scores = jnp.where(block_mask, scores, -1e30)
                    top = jnp.max(scores, axis=1, keepdims=True)
                    e = jnp.exp(scores - top)
                    weight = (e / jnp.sum(e, axis=1, keepdims=True)).astype(BF)
                    prob[layer, g * pairs + p] = weight
                    o = mm(
                        jnp.concatenate([weight[:LANES], weight[LANES:]], 1),
                        split_rows(v, half_mask).astype(BF),
                    )
                    c_o[layer, rs, p * LANES : (p + 1) * LANES] = o.astype(BF)
            y = x_ref[...] + mm(c_o[layer], w_in[layer, :, 3 * d : 4 * d])
            y_ref[...] = y
            normed, scale = norm_forward(y)
            u2 = normed.astype(BF)
            c_u2[layer] = u2
            r2[layer] = scale
            for part in range(ff // chunk):
                cs = slice(part * chunk, (part + 1) * chunk)
                pre = mm(u2, w_in[layer, :, 4 * d + part * chunk : 4 * d + (part + 1) * chunk])
                square = pre * pre
                t = jnp.tanh(GELU_A * pre * (1.0 + GELU_B * square))
                half = 0.5 * (1.0 + t)
                c_h[layer, :, cs] = (pre * half).astype(BF)
                slope = half + 0.5 * pre * (1.0 - t * t) * (GELU_A * (1.0 + 3.0 * GELU_B * square))
                gp[layer, :, cs] = slope.astype(BF)
            x_ref[...] = y_ref[...] + mm(c_h[layer], w_down[layer])

            @pl.when(layer == 0)
            def _():
                cut = x_ref[...].astype(BF).astype(F32)
                x_ref[...] = jnp.where(row_slot < filled, cut, 0.0)

            return carry

        lax.fori_loop(0, layers, forward, 0)

        pooled = jnp.mean(x_ref[...].reshape(images, tok, d), axis=1)
        pnorm, pscale = norm_forward(pooled)
        pb = pnorm.astype(BF)
        here = lax.broadcasted_iota(jnp.int32, classifier.shape, 1) == shard
        weights_cls = jnp.sum(jnp.where(here, classifier[...].astype(F32), 0.0), axis=1).astype(BF)
        logits = mm_nt(pb, weights_cls)
        image = lax.broadcasted_iota(jnp.int32, (images, 1), 0)
        label = jnp.zeros((images, 1), jnp.int32)
        for n in range(images):
            k, i = n // per_image, n % per_image
            value = labels[slot[k] * cfg["img"] + rank * per_image + i]
            label = jnp.where(image == n, value, label)
        full = (image // per_image < filled).astype(F32)
        hot = (lax.broadcasted_iota(jnp.int32, (images, classes), 1) == label).astype(F32)
        top = jnp.max(logits, axis=1, keepdims=True)
        e = jnp.exp(logits - top)
        total = jnp.sum(e, axis=1, keepdims=True)
        picked = jnp.sum(hot * logits, axis=1, keepdims=True)
        loss = (jnp.log(total) + top - picked) * full
        diagonal = lax.broadcasted_iota(jnp.int32, (images, images), 1) == image
        losses[...] = jnp.sum(jnp.where(diagonal, loss, 0.0), axis=0, keepdims=True)
        dlogits = ((e / total - hot) * full).astype(BF)
        dcls[...] = mm_tn(dlogits, pb)
        dpb = mm(dlogits, weights_cls).astype(BF).astype(F32)
        dpool = norm_backward(dpb, pnorm, pscale) * (1.0 / tok)
        x_ref[...] = jnp.broadcast_to(dpool[:, None, :], (images, tok, d)).reshape(rows, d)

        def backward(step, carry):
            layer = layers - 1 - step
            dout = x_ref[...]
            dob = dout.astype(BF)
            c_dout[layer] = dob
            for part in range(ff // chunk):
                cs = slice(part * chunk, (part + 1) * chunk)
                dh = mm_nt(dob, w_down[layer, cs]).astype(BF).astype(F32)
                c_dpre[layer, :, cs] = (dh * gp[layer, :, cs].astype(F32)).astype(BF)
            du2 = mm_nt(c_dpre[layer], w_in[layer, :, 4 * d :]).astype(BF).astype(F32)
            dy = x_ref[...] + norm_backward(du2, c_u2[layer].astype(F32), r2[layer])
            y_ref[...] = dy
            dyb = dy.astype(BF)
            c_dy[layer] = dyb
            do = mm_nt(dyb, w_in[layer, :, 3 * d : 4 * d]).astype(BF).astype(F32)
            head_dim = d // HEADS
            for g in range(halves):
                rs = slice(g * LANES, (g + 1) * LANES)
                for p in range(pairs):
                    ls = slice(p * LANES, (p + 1) * LANES)
                    d2 = split_rows(do[rs, ls], half_mask).astype(BF)
                    q = qkv_b[layer, rs, p * LANES : (p + 1) * LANES].astype(F32)
                    k = qkv_b[layer, rs, d + p * LANES : d + (p + 1) * LANES].astype(F32)
                    v = qkv_b[layer, rs, 2 * d + p * LANES : 2 * d + (p + 1) * LANES]
                    weight = prob[layer, g * pairs + p]
                    wide = weight.astype(F32)
                    dprob = mm_nt(d2, v)
                    mixed = wide * dprob
                    dscore = mixed - wide * jnp.sum(mixed, axis=1, keepdims=True)
                    dscore = (dscore * (1.0 / math.sqrt(head_dim))).astype(BF)
                    dv = mm_tn(weight, d2)
                    dq = mm(
                        jnp.concatenate([dscore[:LANES], dscore[LANES:]], 1),
                        split_rows(k, half_mask).astype(BF),
                    )
                    dk = mm_tn(dscore, split_rows(q, half_mask).astype(BF))
                    c_dqkv[layer, rs, p * LANES : (p + 1) * LANES] = dq.astype(BF)
                    c_dqkv[layer, rs, d + p * LANES : d + (p + 1) * LANES] = dk.astype(BF)
                    c_dqkv[layer, rs, 2 * d + p * LANES : 2 * d + (p + 1) * LANES] = dv.astype(BF)
            du = mm_nt(c_dqkv[layer], w_in[layer, :, : 3 * d]).astype(BF).astype(F32)
            dx = y_ref[...] + norm_backward(du, c_u[layer].astype(F32), r1[layer])
            x_ref[...] = dx

            @pl.when(layer == 1)
            def _():
                x_ref[...] = x_ref[...].astype(BF).astype(F32)

            for which in range(1, layers):

                @pl.when(layer == which)
                def _(which=which):
                    for copy in saved_copies(which):
                        copy.start()

            return carry

        lax.fori_loop(0, layers, backward, 0)

        chip = me // 2

        def emit(values, at):
            for n in sorted(values)[::2]:
                own = jnp.where(core == 0, values[n], values[n + 1])
                other = jnp.where(core == 0, values[n + 1], values[n])
                keep[slot_of_chip(chip ^ (n // 2), core, bits), at] = own.astype(BF)
                send[slot_of_chip(chip ^ (n // 2), 1 - core, bits), at] = other.astype(BF)

        def emit_columns(first, cot, act):
            value = mm_tn(cot, act)
            count = value.shape[0] // cin
            base = first // cin
            emit(
                {base + i: value[i * cin : (i + 1) * cin] for i in range(count)},
                slice(0, cin),
            )

        width = members * ROWS16
        column = lax.broadcasted_iota(jnp.int32, (d, width), 1)
        row = lax.broadcasted_iota(jnp.int32, (d, width), 0)
        inner = column % ROWS16
        sel = ((inner < dpc) & (row == (column // ROWS16) * dpc + inner)).astype(BF)
        dob_pad[...] = mm(c_dout[0], sel).astype(BF)
        for part in range(ff // d):
            value = mm_tn(dob_pad[...], c_h[0, :, part * d : (part + 1) * d])
            emit(
                {n: value[n * ROWS16 : (n + 1) * ROWS16] for n in range(members)},
                slice(cin_pad + part * ROWS16, cin_pad + (part + 1) * ROWS16),
            )
        copies = grad_copies(0, cin_pad, (ff // d) * ROWS16)
        for copy in copies:
            copy.start()
        for part in range(3):
            emit_columns(part * d, c_dqkv[0, :, part * d : (part + 1) * d], c_u[0])
        emit_columns(3 * d, c_dy[0], c_o[0])
        for part in range(ff // d):
            emit_columns(4 * d + part * d, c_dpre[0, :, part * d : (part + 1) * d], c_u2[0])

        copies += grad_copies(1, 0, cin_pad)
        for copy in copies[2:]:
            copy.start()
        dob_pad[...] = mm(x_ref[...].astype(BF), sel).astype(BF)
        value = jnp.concatenate([mm(pcat[...], dob_pad[...]), jnp.zeros((d - patch - tok, width), F32)], 0).T
        base = cin_pad + (ff // d) * ROWS16
        emit(
            {n: value[n * ROWS16 : (n + 1) * ROWS16] for n in range(members)},
            slice(base, base + ROWS16),
        )
        copies += grad_copies(2, base, ROWS16)
        for copy in copies[4:]:
            copy.start()
        for layer in range(1, layers):
            copies += saved_copies(layer)
        for copy in copies:
            copy.wait()

    height = cin_pad + (ff // d) * ROWS16 + ROWS16
    cfg["height"] = height
    wide = 4 * d + ff
    saved = [d, d, d, ff, 3 * d, d, ff, d]
    out_shape = [
        jax.ShapeDtypeStruct((1, images), F32),
        jax.ShapeDtypeStruct((classes, d), F32),
        jax.ShapeDtypeStruct((chips, height, d), BF),
        jax.ShapeDtypeStruct((chips, height, d), BF),
    ] + [jax.ShapeDtypeStruct((layers - 1, rows, w), BF) for w in saved]
    any_spec = pl.BlockSpec(memory_space=pl.ANY)
    smem = pl.BlockSpec(memory_space=pltpu.SMEM)
    vmem = pl.BlockSpec(memory_space=pltpu.VMEM)
    n_sems = 2 + (layers - 1) * 2 * group + capacity + (layers - 1) * 8 + 6
    scratch = [
        pltpu.VMEM((layers, d, wide), BF),
        pltpu.VMEM((layers, ff, d), BF),
        pltpu.VMEM((capacity, packed, LANES), BF),
        pltpu.SMEM((capacity,), jnp.int32),
        pltpu.VMEM((rows, d), F32),
        pltpu.VMEM((rows, d), F32),
        pltpu.VMEM((rows, 3 * d), F32),
        pltpu.VMEM((layers, rows, 3 * d), BF),
        pltpu.VMEM((layers, halves * pairs, 2 * LANES, LANES), BF),
        pltpu.VMEM((layers, rows, ff), BF),
        pltpu.VMEM((layers, rows, 1), F32),
        pltpu.VMEM((layers, rows, 1), F32),
    ]
    scratch += [pltpu.VMEM((layers, rows, w), BF) for w in saved]
    scratch += [
        pltpu.VMEM((patch + tok, rows), BF),
        pltpu.VMEM((rows, members * ROWS16), BF),
        pltpu.VMEM((chips, height, d), BF),
        pltpu.VMEM((chips, height, d), BF),
        pltpu.SemaphoreType.DMA((n_sems,)),
    ]
    n_any = 2 * len(pieces)
    return pl.pallas_call(
        kernel,
        name="chain",
        in_specs=[smem, smem, any_spec, vmem, vmem, any_spec, any_spec]
        + [any_spec] * n_any
        + [vmem],
        out_specs=[vmem, vmem] + [any_spec] * (len(out_shape) - 2),
        out_shape=out_shape,
        scratch_shapes=scratch,
        compiler_params=pltpu.CompilerParams(vmem_limit_bytes=58 * 1024 * 1024),
    )


def make_pack(cfg):
    members, group, patch = cfg["members"], cfg["group"], cfg["patch"]
    packed, width = patch // group, LANES // group

    def kernel(patches, out):
        lane = lax.broadcasted_iota(jnp.int32, (packed, LANES), 1)
        parts = [patches[s * packed : (s + 1) * packed].astype(F32) for s in range(group)]
        for j in range(group):
            value = parts[0]
            for s in range(group):
                moved = pltpu.roll(parts[s], (width * (s - j)) % LANES, 1)
                value = jnp.where(lane // width == s, moved, value)
            value = value.astype(BF)
            for shard in range(members // group):
                out[shard * group + j] = value

    return pl.pallas_call(
        kernel, name="pack", out_shape=jax.ShapeDtypeStruct((members, packed, LANES), BF)
    )


def make_server_grads(cfg):
    d, ff, group, layers = cfg["d"], cfg["ff"], cfg["group"], cfg["layers"]
    rows_in, rows_down = d // group, ff // group
    wide = 4 * d + ff
    half = group // 2

    def kernel(u, o, u2, h, dqkv, dy, dpre, dout, k_in, s_in, k_down, s_down, t_in, t_down):
        rank = lax.axis_index("client") % group
        for part in range(3):
            t_in[:, part * d : (part + 1) * d] = mm_tn(u[...], dqkv[:, part * d : (part + 1) * d]).astype(BF)
        t_in[:, 3 * d : 4 * d] = mm_tn(o[...], dy[...]).astype(BF)
        for part in range(ff // d):
            cs = slice(part * d, (part + 1) * d)
            t_in[:, 4 * d + part * d : 4 * d + (part + 1) * d] = mm_tn(u2[...], dpre[:, cs]).astype(BF)
            t_down[cs] = mm_tn(h[:, cs], dout[...]).astype(BF)
        for p in range(group):
            owner = rank ^ p
            o_in, o_down = (k_in, k_down) if p < half else (s_in, s_down)
            o_in[p % half] = t_in[pl.ds(pl.multiple_of(owner * rows_in, rows_in), rows_in)]
            o_down[p % half] = t_down[pl.ds(pl.multiple_of(owner * rows_down, rows_down), rows_down)]

    rows = cfg["capacity"] * cfg["pr"]
    flops = 2 * rows * (d * wide + ff * d) * (layers - 1)
    saved = [d, d, d, ff, 3 * d, d, ff, d]
    in_block = pl.BlockSpec((half, None, rows_in, wide), lambda i: (0, i, 0, 0))
    down_block = pl.BlockSpec((half, None, rows_down, d), lambda i: (0, i, 0, 0))
    return pl.pallas_call(
        kernel,
        name="server_grads",
        grid=(layers - 1,),
        in_specs=[pl.BlockSpec((None, rows, w), lambda i: (i, 0, 0)) for w in saved],
        out_specs=[in_block, in_block, down_block, down_block],
        out_shape=[jax.ShapeDtypeStruct((half, layers - 1, rows_in, wide), BF)] * 2
        + [jax.ShapeDtypeStruct((half, layers - 1, rows_down, d), BF)] * 2,
        scratch_shapes=[pltpu.VMEM((d, wide), BF), pltpu.VMEM((ff, d), BF)],
        cost_estimate=pl.CostEstimate(flops=flops * 4, bytes_accessed=16 * 2**20, transcendentals=0),
        compiler_params=pltpu.CompilerParams(vmem_limit_bytes=48 * 1024 * 1024),
    )


def make_finish(cfg):
    d, ff, tok, patch = cfg["d"], cfg["ff"], cfg["tok"], cfg["patch"]
    members, cin, cin_pad, group = cfg["members"], cfg["cin"], cfg["cin_pad"], cfg["group"]
    classes = cfg["classes"]
    dpc, rows_in = d // members, d // group

    def kernel(a, b, cls, g_embed, g_pos, g_in, g_down, g_class):
        total = a[0].astype(F32) + b[0].astype(F32)
        g_in[...] = total[:cin]
        for part in range(ff // d):
            first = cin_pad + part * ROWS16
            g_down[:, part * d : (part + 1) * d] = total[first : first + dpc]
        first = cin_pad + (ff // d) * ROWS16
        g_embed[...] = total[first : first + dpc, :patch]
        g_pos[...] = total[first : first + dpc, patch : patch + tok]
        rank = lax.axis_index("client") % group
        value = cls[:, :rows_in]
        for r in range(1, group):
            value = jnp.where(rank == r, cls[:, r * rows_in : (r + 1) * rows_in], value)
        g_class[...] = value

    return pl.pallas_call(
        kernel,
        name="finish",
        out_shape=[
            jax.ShapeDtypeStruct((dpc, patch), F32),
            jax.ShapeDtypeStruct((dpc, tok), F32),
            jax.ShapeDtypeStruct((cin, d), F32),
            jax.ShapeDtypeStruct((dpc, ff), F32),
            jax.ShapeDtypeStruct((classes, rows_in), F32),
        ],
        compiler_params=pltpu.CompilerParams(vmem_limit_bytes=32 * 1024 * 1024),
    )


def swap_bit(block, bit):
    count = lax.axis_size("client")
    return lax.ppermute(block, "client", [(i, i ^ (1 << bit)) for i in range(count)])


def swap_by_core(block, even, odd):
    count = lax.axis_size("client")
    return lax.ppermute(
        block, "client", [(i, i ^ (1 << (even if i % 2 == 0 else odd))) for i in range(count)]
    )


def per_device(
    patches,
    labels,
    assign,
    patch_embed,
    positions,
    client_in,
    client_down,
    server_in,
    server_down,
    classifier,
):
    members = lax.axis_size("client")
    group = members // SHARDS
    group_bits = group.bit_length() - 1
    bits = members.bit_length() - 1
    patch, d = patch_embed.shape
    tok = positions.shape[0]
    ff = client_down.shape[0]
    img = labels.shape[0] // members
    layers = server_in.shape[0] + 1
    pr = patches.shape[0] // group
    rows_in, rows_down = server_in.shape[1], server_down.shape[1]
    cin = client_in.shape[1] // members
    capacity = SLOTS * group

    pieces, first = [1], [0]
    piece_in, piece_down = [server_in[None]], [server_down[None]]
    for bit in range(group_bits):
        whole_in = piece_in[0] if bit == 0 else jnp.concatenate(piece_in, 0)
        whole_down = piece_down[0] if bit == 0 else jnp.concatenate(piece_down, 0)
        piece_in.append(swap_bit(whole_in, bit))
        piece_down.append(swap_bit(whole_down, bit))
        first.append(1 << bit)
        pieces.append(1 << bit)

    cfg = dict(
        d=d,
        ff=ff,
        tok=tok,
        patch=patch,
        members=members,
        group=group,
        capacity=capacity,
        pr=pr,
        images=capacity * pr // tok,
        classes=classifier.shape[2],
        layers=layers,
        bits=bits,
        cin=cin,
        cin_pad=-(-cin // ROWS16) * ROWS16,
        pieces=pieces,
        first=first,
        packed=patch // group,
        img=img,
    )
    outgoing = make_pack(cfg)(patches.T)
    arrived = lax.all_to_all(outgoing, "client", split_axis=0, concat_axis=0, tiled=True)
    results = make_chain(cfg)(
        assign.reshape(-1),
        labels,
        arrived,
        patch_embed,
        positions,
        client_in,
        client_down,
        *piece_in,
        *piece_down,
        classifier.transpose(2, 0, 1),
    )
    losses, dcls, keep, send = results[:4]
    saved = results[4:]

    even, odd = stage_orders(bits)
    recv = swap_bit(send, 0)
    for step in range(bits - 1):
        half = keep.shape[0] // 2
        send = (keep[half:].astype(F32) + recv[half:].astype(F32)).astype(BF)
        keep = (keep[:half].astype(F32) + recv[:half].astype(F32)).astype(BF)
        recv = swap_by_core(send, even[step], odd[step])

    keep_in, send_in, keep_down, send_down = make_server_grads(cfg)(*saved)
    for bit in range(group_bits - 1, -1, -1):
        got_in = keep_in.astype(F32) + swap_bit(send_in, bit).astype(F32)
        got_down = keep_down.astype(F32) + swap_bit(send_down, bit).astype(F32)
        half = got_in.shape[0] // 2
        keep_in, send_in = got_in[:half], got_in[half:].astype(BF)
        keep_down, send_down = got_down[:half], got_down[half:].astype(BF)
    for bit in range(group_bits):
        dcls = dcls + swap_bit(dcls, bit)
    g_embed, g_pos, g_client_in, g_client_down, g_class = make_finish(cfg)(keep, recv, dcls)

    return (
        losses,
        g_embed.T,
        g_pos.T,
        g_client_in.T,
        g_client_down.T,
        got_in[0],
        got_down[0],
        g_class.T,
    )


def solution(mesh):
    in_specs = (
        P("client", None),
        P(),
        P(),
        P(),
        P(),
        P(),
        P(),
        P(None, "client", None),
        P(None, "client", None),
        P(),
    )
    out_specs = (
        P("client", None),
        P(None, "client"),
        P(None, "client"),
        P(None, "client"),
        P(None, "client"),
        P(None, "client", None),
        P(None, "client", None),
        P("client", None),
    )
    return jax.shard_map(
        per_device, mesh=mesh, in_specs=in_specs, out_specs=out_specs, check_vma=False
    )
```

time: 723 us -> 115 us (0.16)
  local copies, waits for them, and re-layouts: 242 us -> 2.37 us
  other arithmetic: 157 us -> 7.51 us
  blocking collectives: 123 us -> 0 us
  matrix products: 75.8 us -> 0 us
  Pallas kernels: 0 us -> 42.8 us
  starting transfers between devices: 34.4 us -> 13.8 us
  waiting for transfers between devices: 67 us -> 47.8 us
  between operations: 17.3 us -> 0.73 us
    unnamed x2 -> x0, blocking collectives: 123 us -> none
    slice x7 -> x0, local copies, waits for them, and re-layouts: 87.6 us -> none  [the longest x1 52 us: per_device(): own_sum[:size_in].reshape(SERVER_LAYERS, rows_in, width_all)]
    dot_general x62 -> x0, matrix products: 75.8 us -> none  [the longest x9 13.8 us: encoder_block(): jnp.dot(normed, weight_in[:, 4 * model_width:], preferred_element_type=jn...]
    unnamed x12 -> x0, waiting for transfers between devices: 67 us -> none
    concatenate x2 -> x0, other arithmetic: 66.5 us -> none  [the longest x1 56.1 us: per_device(): blocks = jnp.concatenate([blocks_in, blocks_down, blocks_class], 1)]
    pallas_call x0 -> x4, Pallas kernels: none -> 42.8 us  [the longest x1 34 us: per_device(): make_chain(cfg)]
    broadcast_in_dim x2 -> x0, local copies, waits for them, and re-layouts: 41.6 us -> none  [the longest x1 41.6 us: gather_group(): stacked = flat_rows[None]]
    select_n x3 -> x0, other arithmetic: 34.4 us -> none  [the longest x1 33 us: gather_group(): jnp.where(upper_half == 0, jnp.concatenate([stacked, partner], 0), jnp.co...]
  transfers between devices with their start and end apart: 14 -> 11, of which waited for: 2 -> 8; matrix products, arithmetic and copies ran while one was open for 52% -> 5% of each run, Pallas kernels for 0% -> 7%
where the time goes in v1:
time: 115 us
  waiting for transfers between devices  47.8 us (42%)
  Pallas kernels  42.8 us (37%)
  starting transfers between devices  13.8 us (12%)
  other arithmetic  7.51 us (7%)
  local copies, waits for them, and re-layouts  2.37 us (2%)
    pallas_call x1, Pallas kernels, per_device(): make_chain(cfg)  34 us
    ppermute x4, waiting for transfers between devices, swap_by_core(): lax.ppermute(block, 'client', [(i, i ^ 1 << (even if i % 2 == 0 else odd)...  21.9 us
    all_to_all x1, waiting for transfers between devices, per_device(): lax.all_to_all(outgoing, 'client', split_axis=0, concat_axis=0, tiled=True)  17.3 us
    ppermute x6, waiting for transfers between devices, swap_bit(): lax.ppermute(block, 'client', [(i, i ^ 1 << bit) for i in range(count)])  8.59 us
    all_to_all x1, starting transfers between devices, per_device(): lax.all_to_all(outgoing, 'client', split_axis=0, concat_axis=0, tiled=True)  6.95 us
    pallas_call x1, Pallas kernels, per_device(): keep_in, send_in, keep_down, send_down = make_server_grads(cfg)(*saved)  6.12 us
    ppermute x4, starting transfers between devices, swap_by_core(): lax.ppermute(block, 'client', [(i, i ^ 1 << (even if i % 2 == 0 else odd)...  5.44 us
    squeeze x1, other arithmetic, per_device(): got_in[0]  3.04 us
  transfers between devices with their start and end apart: 11, of which 8 were waited for; matrix products, arithmetic and copies ran while one was open for 5% of the time, Pallas kernels for 7%

profile of v1, /device:TPU:0, one launch (start us, length us, event | category | flops | bytes accessed | tf_op | source)
XLA Modules:
  0.0 115.0 jit_solution(11018682990160522117)
XLA Ops:
  0.6 0.6 collective-permute-start
  1.2 1.8 %pack.1 = bf16[32,96,128]{2,1,0:T(8,128)(2,1)} custom-call(bf16[192,128]{1,0:T(8,128)(2,1)} %bitcast.20), custom_call_target="tpu_custom_call" | custom-call | tf_op jit(solution)/shard_map/pack/pallas_call | solution.py:628
  3.0 6.9 %all-to-all-start = ((bf16[32,96,128]{2,1,0:T(8,128)(2,1)}), bf16[32,96,128]{2,1,0:T(8,128)(2,1)S(1)}, u32[]{:S(2)}, u32[]{:S(2)}) async-start(bf16[32,96,128]{2,1,0:T(8,128)(2,1)} %pack.1), calls=%async_computation | async-start | bytes 1572864 | tf_op jit(solution)/shard_map/all_to_all | solution.py:629
  10.0 0.3 collective-permute-start.1
  10.3 2.9 %collective-permute-done.1.refs_10_ = bf16[1,2,768,384]{3,2,1,0:T(8,128)(2,1)} collective-permute-done((bf16[1,2,768,384]{3,2,1,0:T(8,128)(2,1)}, bf16[1,2,768,384]{3,2,1,0:T(8,128)(2,1)}, u32[]{:S(2)}, u32[]{:S(2)}) %collective-permute-start.1) | collective-permute-done | bytes 1179680 | tf_op jit(solution)/shard_map/ppermute | solution.py:562
  13.2 17.3 %all-to-all-done.refs_2_ = bf16[32,96,128]{2,1,0:T(8,128)(2,1)S(1)} async-done(((bf16[32,96,128]{2,1,0:T(8,128)(2,1)}), bf16[32,96,128]{2,1,0:T(8,128)(2,1)S(1)}, u32[]{:S(2)}, u32[]{:S(2)}) %all-to-all-start) | async-done | bytes 786464 | tf_op jit(solution)/shard_map/all_to_all | solution.py:629
  30.6 0.9 copy-done.6
  31.5 0.7 copy-done.8
  32.2 34.0 %chain.1 = (f32[1,16]{1,0:T(1,128)}, f32[10,384]{1,0:T(8,128)}, bf16[16,176,384]{2,1,0:T(8,128)(2,1)}, bf16[16,176,384]{2,1,0:T(8,128)(2,1)}, bf16[2,256,384]{2,...) custom-call(s32[32]{0:T(128)} %bitcast.21, ...), custom_call_target="tpu_custom_call" | custom-call | tf_op jit(solution)/shard_map/chain/pallas_call | solution.py:630
  66.3 0.1 collective-permute-start.2
  66.3 4.5 %collective-permute-done.2 = bf16[16,176,384]{2,1,0:T(8,128)(2,1)S(1)} collective-permute-done((bf16[16,176,384]{2,1,0:T(8,128)(2,1)}, bf16[16,176,384]{2,1,0:T(8,128)(2,1)S(1)}, u32[]{:S(2)}, u32[]{:S(2)}) %collective-permute-start.2) | collective-permute-done | bytes 2162720 | tf_op jit(solution)/shard_map/ppermute | solution.py:562
  70.8 2.3 %add_convert_fusion.1 = (bf16[8,176,384]{2,1,0:T(8,128)(2,1)S(1)}, bf16[8,176,384]{2,1,0:T(8,128)(2,1)S(1)}) fusion(bf16[16,176,384]{2,1,0:T(8,128)(2,1)S(1)} %collective-permute-done.2, bf16[16,176,384]{2,1,0:T(8,128)(2,1)} %get-tuple-element.30), kind=kLoop, calls=%fused_computation.3 | loop fusion | flops 4325376 | bytes 6488064 | tf_op jit(solution)/shard_map/convert_element_type | solution.py:650
  73.1 1.5 %collective-permute-start.3 = (bf16[8,176,384]{2,1,0:T(8,128)(2,1)S(1)}, bf16[8,176,384]{2,1,0:T(8,128)(2,1)S(1)}, u32[]{:S(2)}, u32[]{:S(2)}) collective-permute-start(bf16[8,176,384]{2,1,0:T(8,128)(2,1)S(1)} %get-tuple-element.59), channel_id=1, source_target_pairs={{0,2},{1,9},{2,0},{3,11},{4,6},{5,13},{6,4},{7,15},{8,10},{9,1},{1... | collective-permute-start | bytes 3244040 | tf_op jit(solution)/shard_map/ppermute | solution.py:567
  74.6 6.1 %server_grads.1 = (bf16[1,2,192,3072]{3,2,1,0:T(8,128)(2,1)}, bf16[1,2,192,3072]{3,2,1,0:T(8,128)(2,1)}, bf16[1,2,768,384]{3,2,1,0:T(8,128)(2,1)S(1)}, bf16[1,2,768,384]{3,2,1,0:T(8,128)(2,1)S(1)}) custom-call(bf16[2,256,384]{2,1,0:T(8,128)(2,1)S(1)} %copy-done.1, bf16[2,256,384]{2,1,0:T(8,128)(2,1)S(1)} %copy-done.2, bf16[2,256,384]{2,1,0:T(8,128)(2,1)S(1)} %copy-done.3, ...), custom_call_target="tpu_custom_call" | custom-call | flops 7247757312 | bytes 16777216 | tf_op jit(solution)/shard_map/server_grads/pallas_call | solution.py:653
  80.8 0.0 collective-permute-start.8
  80.8 0.5 collective-permute-start.9
  81.3 7.0 %collective-permute-done.3 = bf16[8,176,384]{2,1,0:T(8,128)(2,1)S(1)} collective-permute-done((bf16[8,176,384]{2,1,0:T(8,128)(2,1)S(1)}, bf16[8,176,384]{2,1,0:T(8,128)(2,1)S(1)}, u32[]{:S(2)}, u32[]{:S(2)}) %collective-permute-start.3) | collective-permute-done | bytes 1081376 | tf_op jit(solution)/shard_map/ppermute | solution.py:567
  88.3 0.3 add_convert_fusion.3
  88.6 1.6 %collective-permute-start.4 = (bf16[4,176,384]{2,1,0:T(8,128)(2,1)S(1)}, bf16[4,176,384]{2,1,0:T(8,128)(2,1)S(1)}, u32[]{:S(2)}, u32[]{:S(2)}) collective-permute-start(bf16[4,176,384]{2,1,0:T(8,128)(2,1)S(1)} %get-tuple-element.61), channel_id=1, source_target_pairs={{0,4},{1,3},{2,6},{3,1},{4,0},{5,7},{6,2},{7,5},{8,12},{9,11},{10,... | collective-permute-start | bytes 1622024 | tf_op jit(solution)/shard_map/ppermute | solution.py:567
  90.2 1.2 %collective-permute-done.7 = f32[10,384]{1,0:T(8,128)S(1)} collective-permute-done((f32[10,384]{1,0:T(8,128)S(1)}, f32[10,384]{1,0:T(8,128)S(1)}, u32[]{:S(2)}, u32[]{:S(2)}) %collective-permute-start.7) | collective-permute-done | bytes 15392 | tf_op jit(solution)/shard_map/ppermute | solution.py:562
  91.4 6.6 %collective-permute-done.4 = bf16[4,176,384]{2,1,0:T(8,128)(2,1)S(1)} collective-permute-done((bf16[4,176,384]{2,1,0:T(8,128)(2,1)S(1)}, bf16[4,176,384]{2,1,0:T(8,128)(2,1)S(1)}, u32[]{:S(2)}, u32[]{:S(2)}) %collective-permute-start.4) | collective-permute-done | bytes 540704 | tf_op jit(solution)/shard_map/ppermute | solution.py:567
  98.0 0.1 add_convert_fusion.5
  98.2 1.5 %collective-permute-start.5 = (bf16[2,176,384]{2,1,0:T(8,128)(2,1)S(1)}, bf16[2,176,384]{2,1,0:T(8,128)(2,1)S(1)}, u32[]{:S(2)}, u32[]{:S(2)}) collective-permute-start(bf16[2,176,384]{2,1,0:T(8,128)(2,1)S(1)} %get-tuple-element.63), channel_id=1, source_target_pairs={{0,8},{1,17},{2,10},{3,19},{4,12},{5,21},{6,14},{7,23},{8,0},{9,25... | collective-permute-start | bytes 811016 | tf_op jit(solution)/shard_map/ppermute | solution.py:567
  99.6 0.0 collective-permute-done.9
  99.7 1.7 %add_bitcast_fusion.1 = f32[2,768,384]{2,1,0:T(8,128)} fusion(bf16[1,2,768,384]{3,2,1,0:T(8,128)(2,1)S(1)} %collective-permute-done.9, bf16[1,2,768,384]{3,2,1,0:T(8,128)(2,1)S(1)} %get-tuple-element.47), kind=kLoop, calls=%fused_computation.1 | loop fusion | flops 1769472 | bytes 4718592 | tf_op jit(solution)/shard_map/squeeze | solution.py:671
  101.4 5.3 %collective-permute-done.5 = bf16[2,176,384]{2,1,0:T(8,128)(2,1)S(1)} collective-permute-done((bf16[2,176,384]{2,1,0:T(8,128)(2,1)S(1)}, bf16[2,176,384]{2,1,0:T(8,128)(2,1)S(1)}, u32[]{:S(2)}, u32[]{:S(2)}) %collective-permute-start.5) | collective-permute-done | bytes 270368 | tf_op jit(solution)/shard_map/ppermute | solution.py:567
  106.6 0.1 add_convert_fusion.6
  106.7 0.9 collective-permute-start.6
  107.5 3.0 %add_bitcast_fusion = f32[2,192,3072]{2,1,0:T(8,128)} fusion(bf16[1,2,192,3072]{3,2,1,0:T(8,128)(2,1)S(1)} %collective-permute-done.8, bf16[1,2,192,3072]{3,2,1,0:T(8,128)(2,1)S(1)} %copy-done.7), kind=kLoop, calls=%fused_computation | loop fusion | flops 3538944 | bytes 9437184 | tf_op jit(solution)/shard_map/squeeze | solution.py:670
  110.6 3.0 %collective-permute-done.6.b = bf16[1,176,384]{2,1,0:T(8,128)(2,1)S(1)} collective-permute-done((bf16[1,176,384]{2,1,0:T(8,128)(2,1)S(1)}, bf16[1,176,384]{2,1,0:T(8,128)(2,1)S(1)}, u32[]{:S(2)}, u32[]{:S(2)}) %collective-permute-start.6) | collective-permute-done | bytes 135200 | tf_op jit(solution)/shard_map/ppermute | solution.py:567
  113.6 0.8 finish.1
  114.3 0.7 copy.18
  (22 shorter events, 0.0 us)
Async XLA Ops:
  0.6 29.9 %collective-permute-start = (bf16[1,2,192,3072]{3,2,1,0:T(8,128)(2,1)}, bf16[1,2,192,3072]{3,2,1,0:T(8,128)(2,1)S(1)}, u32[]{:S(2)}, u32[]{:S(2)}) collective-permute-start(bf16[1,2,192,3072]{3,2,1,0:T(8,128)(2,1)} %bitcast.15), channel_id=1, source_target_pairs={{0,1},{1,0},{2,3},{3,2},{4,5},{5,4},{6,7},{7,6},{8,9},{9,8},{10,11... | collective-permute-start | bytes 7077896 | tf_op jit(solution)/shard_map/ppermute | solution.py:562
  3.0 27.5 %all-to-all-start = ((bf16[32,96,128]{2,1,0:T(8,128)(2,1)}), bf16[32,96,128]{2,1,0:T(8,128)(2,1)S(1)}, u32[]{:S(2)}, u32[]{:S(2)}) async-start(bf16[32,96,128]{2,1,0:T(8,128)(2,1)} %pack.1), calls=%async_computation | async-start | bytes 1572864 | tf_op jit(solution)/shard_map/all_to_all | solution.py:629
  10.0 3.3 %collective-permute-start.1 = (bf16[1,2,768,384]{3,2,1,0:T(8,128)(2,1)}, bf16[1,2,768,384]{3,2,1,0:T(8,128)(2,1)}, u32[]{:S(2)}, u32[]{:S(2)}) collective-permute-start(bf16[1,2,768,384]{3,2,1,0:T(8,128)(2,1)} %bitcast.17), channel_id=1, source_target_pairs={{0,1},{1,0},{2,3},{3,2},{4,5},{5,4},{6,7},{7,6},{8,9},{9,8},{10,11... | collective-permute-start | bytes 3538952 | tf_op jit(solution)/shard_map/ppermute | solution.py:562
  30.6 0.9 copy-start.6
  30.6 1.7 %copy-start.8 = (bf16[1,2,192,3072]{3,2,1,0:T(8,128)(2,1)}, bf16[1,2,192,3072]{3,2,1,0:T(8,128)(2,1)S(1)}, u32[]{:S(2)}) copy-start(bf16[1,2,192,3072]{3,2,1,0:T(8,128)(2,1)S(1)} %collective-permute-done.refs_8_) | copy-start | bytes 7077892
  66.3 4.5 %collective-permute-start.2 = (bf16[16,176,384]{2,1,0:T(8,128)(2,1)}, bf16[16,176,384]{2,1,0:T(8,128)(2,1)S(1)}, u32[]{:S(2)}, u32[]{:S(2)}) collective-permute-start(bf16[16,176,384]{2,1,0:T(8,128)(2,1)} %get-tuple-element.31), channel_id=1, source_target_pairs={{0,1},{1,0},{2,3},{3,2},{4,5},{5,4},{6,7},{7,6},{8,9},{9,8},{10,11... | collective-permute-start | bytes 6488072 | tf_op jit(solution)/shard_map/ppermute | solution.py:562
  70.8 3.8 %copy-start = (bf16[2,256,1152]{2,1,0:T(8,128)(2,1)S(1)}, bf16[2,256,1152]{2,1,0:T(8,128)(2,1)}, u32[]{:S(2)}) copy-start(bf16[2,256,1152]{2,1,0:T(8,128)(2,1)} %get-tuple-element.41.dqkv) | copy-start | bytes 3538948
  70.8 3.8 %copy-start.1 = (bf16[2,256,384]{2,1,0:T(8,128)(2,1)S(1)}, bf16[2,256,384]{2,1,0:T(8,128)(2,1)}, u32[]{:S(2)}) copy-start(bf16[2,256,384]{2,1,0:T(8,128)(2,1)} %get-tuple-element.37.u) | copy-start | bytes 1179652
  70.8 3.8 %copy-start.2 = (bf16[2,256,384]{2,1,0:T(8,128)(2,1)S(1)}, bf16[2,256,384]{2,1,0:T(8,128)(2,1)}, u32[]{:S(2)}) copy-start(bf16[2,256,384]{2,1,0:T(8,128)(2,1)} %get-tuple-element.38.o) | copy-start | bytes 1179652
  70.8 3.8 %copy-start.3 = (bf16[2,256,384]{2,1,0:T(8,128)(2,1)S(1)}, bf16[2,256,384]{2,1,0:T(8,128)(2,1)}, u32[]{:S(2)}) copy-start(bf16[2,256,384]{2,1,0:T(8,128)(2,1)} %get-tuple-element.39.u2) | copy-start | bytes 1179652
  70.8 3.8 %copy-start.4 = (bf16[2,256,384]{2,1,0:T(8,128)(2,1)S(1)}, bf16[2,256,384]{2,1,0:T(8,128)(2,1)}, u32[]{:S(2)}) copy-start(bf16[2,256,384]{2,1,0:T(8,128)(2,1)} %get-tuple-element.42.dy) | copy-start | bytes 1179652
  70.8 3.8 %copy-start.5 = (bf16[2,256,384]{2,1,0:T(8,128)(2,1)S(1)}, bf16[2,256,384]{2,1,0:T(8,128)(2,1)}, u32[]{:S(2)}) copy-start(bf16[2,256,384]{2,1,0:T(8,128)(2,1)} %get-tuple-element.44.dout) | copy-start | bytes 1179652
  73.1 15.2 %collective-permute-start.3 = (bf16[8,176,384]{2,1,0:T(8,128)(2,1)S(1)}, bf16[8,176,384]{2,1,0:T(8,128)(2,1)S(1)}, u32[]{:S(2)}, u32[]{:S(2)}) collective-permute-start(bf16[8,176,384]{2,1,0:T(8,128)(2,1)S(1)} %get-tuple-element.59), channel_id=1, source_target_pairs={{0,2},{1,9},{2,0},{3,11},{4,6},{5,13},{6,4},{7,15},{8,10},{9,1},{1... | collective-permute-start | bytes 3244040 | tf_op jit(solution)/shard_map/ppermute | solution.py:567
  80.8 26.8 %collective-permute-start.8 = (bf16[1,2,192,3072]{3,2,1,0:T(8,128)(2,1)}, bf16[1,2,192,3072]{3,2,1,0:T(8,128)(2,1)S(1)}, u32[]{:S(2)}, u32[]{:S(2)}) collective-permute-start(bf16[1,2,192,3072]{3,2,1,0:T(8,128)(2,1)} %get-tuple-element.46), channel_id=1, source_target_pairs={{0,1},{1,0},{2,3},{3,2},{4,5},{5,4},{6,7},{7,6},{8,9},{9,8},{10,11... | collective-permute-start | bytes 7077896 | tf_op jit(solution)/shard_map/ppermute | solution.py:562
  80.8 18.9 %collective-permute-start.9 = (bf16[1,2,768,384]{3,2,1,0:T(8,128)(2,1)S(1)}, bf16[1,2,768,384]{3,2,1,0:T(8,128)(2,1)S(1)}, u32[]{:S(2)}, u32[]{:S(2)}) collective-permute-start(bf16[1,2,768,384]{3,2,1,0:T(8,128)(2,1)S(1)} %get-tuple-element.48), channel_id=1, source_target_pairs={{0,1},{1,0},{2,3},{3,2},{4,5},{5,4},{6,7},{7,6},{8,9},{9,8},{10,11... | collective-permute-start | bytes 3538952 | tf_op jit(solution)/shard_map/ppermute | solution.py:562
  88.3 1.9 %copy-start.9 = (f32[10,384]{1,0:T(8,128)S(1)}, f32[10,384]{1,0:T(8,128)}, u32[]{:S(2)}) copy-start(f32[10,384]{1,0:T(8,128)} %get-tuple-element.32) | copy-start | bytes 46084
  88.6 9.4 %collective-permute-start.4 = (bf16[4,176,384]{2,1,0:T(8,128)(2,1)S(1)}, bf16[4,176,384]{2,1,0:T(8,128)(2,1)S(1)}, u32[]{:S(2)}, u32[]{:S(2)}) collective-permute-start(bf16[4,176,384]{2,1,0:T(8,128)(2,1)S(1)} %get-tuple-element.61), channel_id=1, source_target_pairs={{0,4},{1,3},{2,6},{3,1},{4,0},{5,7},{6,2},{7,5},{8,12},{9,11},{10,... | collective-permute-start | bytes 1622024 | tf_op jit(solution)/shard_map/ppermute | solution.py:567
  90.2 1.2 %collective-permute-start.7 = (f32[10,384]{1,0:T(8,128)S(1)}, f32[10,384]{1,0:T(8,128)S(1)}, u32[]{:S(2)}, u32[]{:S(2)}) collective-permute-start(f32[10,384]{1,0:T(8,128)S(1)} %copy-done.9), channel_id=1, source_target_pairs={{0,1},{1,0},{2,3},{3,2},{4,5},{5,4},{6,7},{7,6},{8,9},{9,8},{10,11... | collective-permute-start | bytes 46088 | tf_op jit(solution)/shard_map/ppermute | solution.py:562
  98.2 8.5 %collective-permute-start.5 = (bf16[2,176,384]{2,1,0:T(8,128)(2,1)S(1)}, bf16[2,176,384]{2,1,0:T(8,128)(2,1)S(1)}, u32[]{:S(2)}, u32[]{:S(2)}) collective-permute-start(bf16[2,176,384]{2,1,0:T(8,128)(2,1)S(1)} %get-tuple-element.63), channel_id=1, source_target_pairs={{0,8},{1,17},{2,10},{3,19},{4,12},{5,21},{6,14},{7,23},{8,0},{9,25... | collective-permute-start | bytes 811016 | tf_op jit(solution)/shard_map/ppermute | solution.py:567
  99.7 7.9 %copy-start.7 = (bf16[1,2,192,3072]{3,2,1,0:T(8,128)(2,1)S(1)}, bf16[1,2,192,3072]{3,2,1,0:T(8,128)(2,1)}, u32[]{:S(2)}) copy-start(bf16[1,2,192,3072]{3,2,1,0:T(8,128)(2,1)} %get-tuple-element.45) | copy-start | bytes 7077892
  106.7 6.9 %collective-permute-start.6 = (bf16[1,176,384]{2,1,0:T(8,128)(2,1)S(1)}, bf16[1,176,384]{2,1,0:T(8,128)(2,1)S(1)}, u32[]{:S(2)}, u32[]{:S(2)}) collective-permute-start(bf16[1,176,384]{2,1,0:T(8,128)(2,1)S(1)} %get-tuple-element.64), channel_id=1, source_target_pairs={{0,16},{1,5},{2,18},{3,7},{4,20},{5,1},{6,22},{7,3},{8,24},{9,13},... | collective-permute-start | bytes 405512 | tf_op jit(solution)/shard_map/ppermute | solution.py:567
